TPU v7x, 32 devices: a whole 2x2x4 slice. The times are simulated.
32 devices in a mesh: row: 8 (over z, x), col: 4 (over y, core).
Axes of the slice: x: 2, y: 2, z: 4, core: 2. Of those that a mesh axis runs over, the one named last changes fastest.
Arguments:
- forward_map: float32 [2048, 16384], P('row', 'col'), may hold values from -0.125 to 0.125
- sensor_weights: float32 [2048], P('row'), may hold values from 0.25 to 4
- sensor_mask: int32 [2048], P('row'), may hold values 0 or 1
Outputs:
- gram_matrix: float32 [16384, 16384], P('row', 'col')
All inputs are finite; a program needn't handle non-finite values. No bound on the sum of `sensor_mask` on one device may be relied on, other than what follows from the above.
Results may differ from a plain program's by a relative error of at most 0.000061.
Values sent between devices are 32-bit elements; how exact they have to be, the bound alone decides.
No kernel may reach another device: no remote copies, remote signals or barrier semaphores. Data moves between devices by JAX's collectives and lax.ppermute only.
A program may use at most 128 MiB of HBM per device.

v0:
```python
import jax
import jax.numpy as jnp
from jax import lax
from jax.sharding import PartitionSpec as P


def contract(left_rows, right_rows):
    return lax.dot_general(
        left_rows,
        right_rows,
        (((0,), (0,)), ((), ())),
        precision=lax.Precision.HIGHEST,
        preferred_element_type=jnp.float32,
    )


def per_device(forward_map, sensor_weights, sensor_mask):
    sensor_scale = sensor_weights * sensor_mask.astype(jnp.float32)
    weighted = forward_map * sensor_scale[:, None]
    gathered = lax.all_gather(weighted, "row", axis=0, tiled=True)
    spread = lax.all_to_all(forward_map, "col", split_axis=0, concat_axis=1, tiled=True)
    regrouped = lax.all_to_all(spread, "row", split_axis=1, concat_axis=0, tiled=True)
    rows_count = lax.axis_size("row")
    cols_count = lax.axis_size("col")
    columns = gathered.shape[1]
    stride_rows = gathered.shape[0] // (rows_count * cols_count)
    permuted = (
        gathered.reshape(rows_count, cols_count, stride_rows, columns)
        .transpose(1, 0, 2, 3)
        .reshape(-1, columns)
    )
    return contract(lax.all_gather(regrouped, "col", axis=0, tiled=True), permuted)


def solution(mesh):
    placed = (P("row", "col"), P("row"), P("row"))
    return jax.shard_map(
        per_device, mesh=mesh, in_specs=placed, out_specs=P("row", "col"), check_vma=False
    )
```

profile of v0, /device:TPU:0, one launch (start us, length us, event | category | flops | bytes accessed | tf_op | source)
XLA Modules:
  0.0 1065.3 jit_solution(8509121159541855739)
XLA Ops:
  6.5 0.0 all-gather.3.cloned.1.call-start
  6.5 0.7 convert_multiply_fusion
  7.2 4.8 broadcast_multiply_fusion
  12.0 0.0 all-gather.3.cloned.1.call-update
  12.0 0.0 all-gather.5.cloned.1.call-start
  12.1 52.6 %all_to_all.35 = f32[4,64,4096]{2,1,0:T(8,128)S(1)} all-to-all(f32[4,64,4096]{2,1,0:T(8,128)} %bitcast.15), channel_id=1, replica_groups=mesh['row'=8,'col'=4] {'col'}, dimensions={0} | all-to-all | bytes 8388608 | tf_op jit(solution)/shard_map/all_to_all | solution.py:21
  64.7 4.7 copy.13
  69.4 5.5 all_to_all.29
  74.9 4.6 copy.14
  79.5 136.9 %all_to_all.36 = f32[64,8,2048]{2,0,1:T(8,128)} all-to-all(f32[64,8,2048]{2,0,1:T(8,128)S(1)} %copy.14), channel_id=1, replica_groups=mesh['row'=8,'col'=4] {'row'}, dimensions={1} | all-to-all | bytes 8388608 | tf_op jit(solution)/shard_map/all_to_all | solution.py:22
  216.4 0.0 all-gather.5.cloned.1.call-update
  216.4 481.1 %all-gather.3.cloned.1.call-done = f32[2048,4096]{1,0:T(8,128)} async-done(((f32[256,4096]{1,0:T(8,128)}), f32[2048,4096]{1,0:T(8,128)}) %all-gather.3.cloned.1.call-update) | async-done | bytes 33554448 | tf_op jit(solution)/shard_map/all_gather | solution.py:20
  697.5 24.4 %copy.12 = f32[4,8,64,4096]{3,2,1,0:T(8,128)} copy(f32[4,8,64,4096]{3,2,0,1:T(8,128)} %bitcast.13) | data formatting | bytes 67108864 | tf_op jit(solution)/shard_map/transpose | solution.py:29
  721.9 83.1 %all-gather.5.cloned.1.call-done = f32[2048,2048]{1,0:T(8,128)} async-done(((f32[512,2048]{1,0:T(8,128)}), f32[2048,2048]{1,0:T(8,128)}) %all-gather.5.cloned.1.call-update) | async-done | bytes 16777232 | tf_op jit(solution)/shard_map/all_gather | solution.py:32
  805.0 222.4 %convolution_bitcast_fusion = f32[2048,4096]{0,1:T(8,128)} fusion(f32[2048,4096]{1,0:T(8,128)} %bitcast.14, f32[2048,2048]{1,0:T(8,128)} %all-gather.5.cloned.1.call-done), kind=kOutput, calls=%fused_computation | convolution fusion | flops 206158430208 | bytes 83886080 | tf_op jit(solution)/shard_map/dot_general | solution.py:8
  1027.4 31.1 %copy.15 = f32[2048,4096]{1,0:T(8,128)} copy(f32[2048,4096]{0,1:T(8,128)} %convolution_bitcast_fusion) | data formatting | bytes 67108864 | tf_op jit(solution)/shard_map/dot_general | solution.py:8
Async XLA Ops:
  6.5 691.0 %all-gather.3.cloned.1.call-start = ((), (), s32[]{:S(2)}) async-start(), calls=%async_computation.2 | async-start | bytes 37748736 | tf_op jit(solution)/shard_map/all_gather | solution.py:20
  12.0 792.9 %all-gather.5.cloned.1.call-start = ((), (), s32[]{:S(2)}) async-start(), calls=%async_computation.3 | async-start | bytes 20971520 | tf_op jit(solution)/shard_map/all_gather | solution.py:32
Sparse Core Ops, SparseCore 0:
  12.2 685.3 all-gather.2
  699.1 105.8 all-gather.4
where the time goes:
time: 1070 us
  waiting for transfers between devices  564 us (53%)
  matrix products  222 us (21%)
  blocking collectives  189 us (18%)
  local copies, waits for them, and re-layouts  70.3 us (7%)
  between operations  13.4 us (1%)
    all_gather x1, waiting for transfers between devices, per_device(): gathered = lax.all_gather(weighted, 'row', axis=0, tiled=True)  481 us
    dot_general x1, matrix products, contract(): lax.dot_general(left_rows, right_rows, (((0,), (0,)), ((), ())), precisio...  222 us
    all_to_all x1, blocking collectives, per_device(): lax.all_to_all(spread, 'row', split_axis=1, concat_axis=0, tiled=True)  137 us
    all_gather x1, waiting for transfers between devices, per_device(): lax.all_gather(regrouped, 'col', axis=0, tiled=True)  83.1 us
    all_to_all x1, blocking collectives, per_device(): lax.all_to_all(forward_map, 'col', split_axis=0, concat_axis=1, tiled=True)  52.6 us
    dot_general x1, local copies, waits for them, and re-layouts, contract(): lax.dot_general(left_rows, right_rows, (((0,), (0,)), ((), ())), precisio...  31.1 us
    transpose x1, local copies, waits for them, and re-layouts, per_device(): permuted = gathered.reshape(rows_count, cols_count, stride_rows, columns)...  24.4 us
  transfers between devices with their start and end apart: 2, of which 2 were waited for; matrix products, arithmetic and copies ran while one was open for 3% of the time, Pallas kernels for 0%

commit v1 on v0

v1 whole, which is shorter than its diff:
```python
import functools

import jax
import jax.numpy as jnp
from jax import lax
from jax.experimental import pallas as pl
from jax.experimental.pallas import tpu as pltpu
from jax.sharding import PartitionSpec as P


INTERPRET = False


def add_kernel(a_ref, b_ref, acc_ref, out_ref, *, chunk):
    def body(step, carry):
        columns = pl.ds(pl.multiple_of(step * chunk, chunk), chunk)
        product = jnp.dot(a_ref[...], b_ref[:, columns], preferred_element_type=jnp.float32)
        out_ref[:, columns] = product if acc_ref is None else acc_ref[:, columns] + product
        return carry

    lax.fori_loop(0, out_ref.shape[1] // chunk, body, 0)


def first_kernel(a_ref, b_ref, out_ref, *, chunk):
    add_kernel(a_ref, b_ref, None, out_ref, chunk=chunk)


def accumulate(acc, a, b):
    depth, width = b.shape
    height = a.shape[0]
    tile = min(height, 256)
    chunk = min(width, 512)
    block = pl.BlockSpec((tile, width), lambda i: (i, 0))
    specs = [
        pl.BlockSpec((tile, depth), lambda i: (i, 0)),
        pl.BlockSpec((depth, width), lambda i: (0, 0)),
    ]
    given = acc is not None
    return pl.pallas_call(
        functools.partial(add_kernel if given else first_kernel, chunk=chunk),
        grid=(height // tile,),
        in_specs=specs + [block] * given,
        out_specs=block,
        out_shape=jax.ShapeDtypeStruct((height, width), jnp.float32),
        input_output_aliases={2: 0} if given else {},
        compiler_params=pltpu.CompilerParams(vmem_limit_bytes=50 * 2**20),
        cost_estimate=pl.CostEstimate(
            flops=2 * height * width * depth,
            bytes_accessed=4 * height * width * (1 + given) + 2 * depth * (height + width),
            transcendentals=0,
        ),
        interpret=INTERPRET,
    )(a, b, *([acc] if given else []))


def halves(x):
    high = lax.reduce_precision(x, 8, 7)
    return high.astype(jnp.bfloat16), (x - high).astype(jnp.bfloat16)


def contribute(acc, left, right):
    left_high, left_low = halves(left)
    right_high, right_low = halves(right)
    a = jnp.concatenate([left_high, left_high, left_low], axis=0).T
    b = jnp.concatenate([right_high, right_low, right_high], axis=0)
    return accumulate(acc, a, b)


def per_layer(forward_map, sensor_weights, sensor_mask):
    rows = lax.axis_size("row")
    cols = lax.axis_size("col")
    row = lax.axis_index("row")
    col = lax.axis_index("col")
    height, width = forward_map.shape
    span = width * cols // rows
    per_col = width // span
    assert per_col * span == width and cols & (cols - 1) == 0

    order = list(range(0, rows, 2)) + list(range(1, rows, 2))[::-1]
    ahead = [(order[i], order[(i + 1) % rows]) for i in range(rows)]
    back = [(there, here) for here, there in ahead]

    source = row // per_col
    offset = (row % per_col) * span

    def spread(piece):
        held = lax.dynamic_slice(piece, (0, offset), (piece.shape[0], span))
        known, bit = 0, cols // 2
        while bit:
            pairs = []
            for r in range(rows):
                origin = r // per_col
                for c in range(cols):
                    if (c ^ origin) & ~known == 0:
                        pairs.append((r * cols + c, r * cols + (c ^ bit)))
            received = lax.ppermute(held, ("row", "col"), pairs)
            has = ((col ^ source) & ~known) == 0
            held = jnp.where(has, held, received)
            known |= bit
            bit //= 2
        return held

    scale = jnp.sqrt(sensor_weights * sensor_mask.astype(jnp.float32))
    index = lax.broadcasted_iota(jnp.int32, (height, height), 0)
    other = lax.broadcasted_iota(jnp.int32, (height, height), 1)
    before = jnp.sum(jnp.where(index < other, sensor_mask[:, None], 0), axis=0)
    count = jnp.sum(sensor_mask)

    def selected(start, amount):
        wanted = start + lax.broadcasted_iota(jnp.int32, (amount, height), 0)
        pick = (before[None, :] == wanted) & (sensor_mask[None, :] != 0)
        return lax.dot_general(
            jnp.where(pick, scale[None, :], 0.0),
            forward_map,
            (((1,), (0,)), ((), ())),
            precision=lax.Precision.HIGHEST,
            preferred_element_type=jnp.float32,
        )

    room = min(height, -(-height * 9 // 256) * 16)
    own = selected(0, room)
    most = lax.pmax(count, "row")
    up, down = own[: room // 2], own[room // 2 :]
    acc = None
    pending = [(spread(own), own)]
    for step in range(1, rows):
        up = lax.ppermute(up, "row", ahead)
        down = lax.ppermute(down, "row", back)
        right = jnp.concatenate([up, down], axis=0)
        pending.append((spread(right), right))
        if len(pending) == 2 or step == rows - 1:
            left = jnp.concatenate([piece for piece, _ in pending], axis=0)
            right = jnp.concatenate([piece for _, piece in pending], axis=0)
            acc = contribute(acc, left, right)
            pending = []

    extra = 16
    if room < height:

        def more(step, total):
            block = selected(room + step * extra, extra)
            gathered = lax.all_gather(block, "row", axis=0, tiled=True)
            return contribute(total, spread(gathered), gathered)

        steps = jnp.maximum(most - room + extra - 1, 0) // extra
        acc = lax.fori_loop(0, steps, more, acc)
    return acc


def solution(mesh):
    placed = (P("row", "col"), P("row"), P("row"))
    return jax.shard_map(
        per_layer, mesh=mesh, in_specs=placed, out_specs=P("row", "col"), check_vma=False
    )
```

time: 1070 us -> 431 us (0.40)
  waiting for transfers between devices: 564 us -> 89.2 us
  matrix products: 222 us -> 4.67 us
  blocking collectives: 189 us -> 28.9 us
  Pallas kernels: 0 us -> 139 us
  starting transfers between devices: 0.04 us -> 51.6 us
  other arithmetic: 5.48 us -> 50.3 us
  local copies, waits for them, and re-layouts: 70.3 us -> 49.9 us
    all_gather x2 -> x0, waiting for transfers between devices: 564 us -> none  [the longest x1 481 us: per_device(): gathered = lax.all_gather(weighted, 'row', axis=0, tiled=True)]
    dot_general x1, matrix products: 222 us -> 4.67 us  [selected(): lax.dot_general(jnp.where(pick, scale[None, :], 0.0), forward_map, (((1,)...]
    all_to_all x2 -> x0, blocking collectives: 189 us -> none  [the longest x1 137 us: per_device(): lax.all_to_all(spread, 'row', split_axis=1, concat_axis=0, tiled=True)]
    pallas_call x0 -> x4, Pallas kernels: none -> 139 us  [accumulate(): pl.pallas_call(functools.partial(add_kernel if given else first_kernel, c...]
    ppermute x0 -> x30, waiting for transfers between devices: none -> 89.2 us  [the longest x7 64.8 us: per_layer(): down = lax.ppermute(down, 'row', back)]
    ppermute x0 -> x30, starting transfers between devices: none -> 51.6 us  [the longest x16 36.1 us: spread(): received = lax.ppermute(held, ('row', 'col'), pairs)]
    dot_general x1 -> x0, local copies, waits for them, and re-layouts: 31.1 us -> none  [contract(): lax.dot_general(left_rows, right_rows, (((0,), (0,)), ((), ())), precisio...]
    pmax x0 -> x1, blocking collectives: none -> 28.9 us  [per_layer(): most = lax.pmax(count, 'row')]
  transfers between devices with their start and end apart: 2 -> 30, of which waited for: 2 -> 14; matrix products, arithmetic and copies ran while one was open for 3% -> 21% of each run, Pallas kernels for 0% -> 24%
where the time goes in v1:
time: 431 us; the launch traced here: 429 us
  Pallas kernels  139 us (32%)
  waiting for transfers between devices  89.2 us (21%)
  starting transfers between devices  51.6 us (12%)
  other arithmetic  50.3 us (12%)
  local copies, waits for them, and re-layouts  49.9 us (12%)
  blocking collectives  28.9 us (7%)
  between operations  14.4 us (3%)
  matrix products  4.67 us (1%)
    pallas_call x4, Pallas kernels, accumulate(): pl.pallas_call(functools.partial(add_kernel if given else first_kernel, c...  139 us
    ppermute x7, waiting for transfers between devices, per_layer(): down = lax.ppermute(down, 'row', back)  64.8 us
    ppermute x16, starting transfers between devices, spread(): received = lax.ppermute(held, ('row', 'col'), pairs)  36.1 us
    pmax x1, blocking collectives, per_layer(): most = lax.pmax(count, 'row')  28.9 us
    unnamed x29, local copies, waits for them, and re-layouts  23.8 us
    ppermute x7, waiting for transfers between devices, per_layer(): up = lax.ppermute(up, 'row', ahead)  18.4 us
    transpose x4, local copies, waits for them, and re-layouts, contribute(): a = jnp.concatenate([left_high, left_high, left_low], axis=0).T  16.3 us
    convert_element_type x8, other arithmetic, halves(): return (high.astype(jnp.bfloat16), (x - high).astype(jnp.bfloat16))  13.6 us
  transfers between devices with their start and end apart: 30, of which 14 were waited for; matrix products, arithmetic and copies ran while one was open for 21% of the time, Pallas kernels for 24%

profile of v1, /device:TPU:0, one launch (start us, length us, event | category | flops | bytes accessed | tf_op | source)
XLA Modules:
  0.0 428.7 jit_solution(7599708219555944635)
XLA Ops:
  8.7 4.7 %fusion.27 = f32[144,4096]{1,0:T(8,128)S(1)} fusion(f32[256,4096]{1,0:T(8,128)} %param.5, f32[256]{0:T(256)S(1)} %multiply_sqrt_fusion, s32[256]{0:T(256)S(1)} %select_reduce_fusion, pred[256]{0:T(512)(128)(4,1)S(1)} %broadcast_compare_fusion.1), kind=kOutput, calls=%fused_computation.99 | convolution fusion | flops 1812049920 | bytes 6555904 | tf_op jit(solution)/shard_map/dot_general | solution.py:112
  13.4 1.6 fusion.36
  15.0 3.0 collective-permute-start.2
  19.2 4.9 %collective-permute-start.28 = (f32[144,2048]{1,0:T(8,128)}, f32[144,2048]{1,0:T(8,128)}, u32[]{:S(2)}, u32[]{:S(2)}) collective-permute-start(f32[144,2048]{1,0:T(8,128)} %constant_dynamic-slice_fusion.1), channel_id=1, source_target_pairs={{0,2},{4,6},{9,11},{13,15},{18,16},{22,20},{27,25},{31,29}} | collective-permute-start | bytes 3538952 | tf_op jit(solution)/shard_map/ppermute | solution.py:96
  24.7 28.9 %pmax.7 = s32[]{:T(128)} all-reduce(s32[]{:T(128)} %reduce_sum.19), channel_id=1, replica_groups=mesh['row'=8,'col'=4] {'row'}, use_global_device_ids=true, to_apply=%region_2.3 | all-reduce | flops 1 | bytes 8 | tf_op jit(solution)/shard_map/pmax | solution.py:122
  55.4 3.5 collective-permute-start.30
  60.7 1.8 collective-permute-start.3
  62.5 2.1 fusion.15
  64.6 3.4 pad_maximum_fusion.4.b_ref
  68.0 4.5 %collective-permute-done.30 = f32[144,2048]{1,0:T(8,128)S(1)} collective-permute-done((f32[144,2048]{1,0:T(8,128)S(1)}, f32[144,2048]{1,0:T(8,128)S(1)}, u32[]{:S(2)}, u32[]{:S(2)}) %collective-permute-start.30) | collective-permute-done | bytes 1179680 | tf_op jit(solution)/shard_map/ppermute | solution.py:96
  74.0 11.0 %collective-permute-done.9 = f32[72,4096]{1,0:T(8,128)} collective-permute-done((f32[72,4096]{1,0:T(8,128)}, f32[72,4096]{1,0:T(8,128)}, u32[]{:S(2)}, u32[]{:S(2)}) %collective-permute-start.9) | collective-permute-done | bytes 1179680 | tf_op jit(solution)/shard_map/ppermute | solution.py:128
  85.0 2.4 fusion.22
  87.4 4.5 %collective-permute-start.24 = (f32[144,2048]{1,0:T(8,128)}, f32[144,2048]{1,0:T(8,128)}, u32[]{:S(2)}, u32[]{:S(2)}) collective-permute-start(f32[144,2048]{1,0:T(8,128)} %fusion.22), channel_id=1, source_target_pairs={{0,2},{4,6},{9,11},{13,15},{18,16},{22,20},{27,25},{31,29}} | collective-permute-start | bytes 3538952 | tf_op jit(solution)/shard_map/ppermute | solution.py:96
  91.8 1.7 collective-permute-start.10
  93.5 2.5 constant_dynamic-update-slice_fusion.11
  96.5 2.4 constant_dynamic-update-slice_fusion.10
  99.9 4.0 copy.14.a_ref
  104.0 15.7 %collective-permute-done.10 = f32[72,4096]{1,0:T(8,128)} collective-permute-done((f32[72,4096]{1,0:T(8,128)}, f32[72,4096]{1,0:T(8,128)}, u32[]{:S(2)}, u32[]{:S(2)}) %collective-permute-start.10) | collective-permute-done | bytes 1179680 | tf_op jit(solution)/shard_map/ppermute | solution.py:128
  119.7 2.6 collective-permute-done.4
  122.2 1.5 fusion.21
  125.1 1.4 broadcast_select_fusion.5
  127.9 33.5 %shard_map.37.acc_ref = f32[2048,4096]{1,0:T(8,128)} custom-call(bf16[2048,864]{1,0:T(8,128)(2,1)S(1)} %copy-done.3, bf16[864,4096]{1,0:T(8,128)(2,1)} %pad_maximum_fusion.4.b_ref), custom_call_target="tpu_custom_call" | custom-call | flops 14495514624 | bytes 44171264 | tf_op jit(solution)/shard_map/pallas_call | solution.py:39
  161.4 2.3 collective-permute-start.11
  163.7 2.4 constant_dynamic-update-slice_fusion.9
  166.1 2.4 constant_dynamic-update-slice_fusion.8
  168.5 3.2 fusion.14
  171.7 3.4 pad_maximum_fusion.3.b_ref
  175.2 1.5 collective-permute-start.27
  176.7 13.3 %collective-permute-done.11 = f32[72,4096]{1,0:T(8,128)} collective-permute-done((f32[72,4096]{1,0:T(8,128)}, f32[72,4096]{1,0:T(8,128)}, u32[]{:S(2)}, u32[]{:S(2)}) %collective-permute-start.11) | collective-permute-done | bytes 1179680 | tf_op jit(solution)/shard_map/ppermute | solution.py:128
  190.1 2.3 fusion.24
  192.4 4.4 %collective-permute-start.20 = (f32[144,2048]{1,0:T(8,128)}, f32[144,2048]{1,0:T(8,128)}, u32[]{:S(2)}, u32[]{:S(2)}) collective-permute-start(f32[144,2048]{1,0:T(8,128)} %fusion.24), channel_id=1, source_target_pairs={{0,2},{4,6},{9,11},{13,15},{18,16},{22,20},{27,25},{31,29}} | collective-permute-start | bytes 3538952 | tf_op jit(solution)/shard_map/ppermute | solution.py:96
  196.8 1.7 collective-permute-start.12
  198.6 2.5 constant_dynamic-update-slice_fusion.7
  201.5 2.4 constant_dynamic-update-slice_fusion.6
  204.9 4.1 copy.15.a_ref
  209.8 1.6 broadcast_select_fusion.7
  212.7 10.2 %collective-permute-done.12 = f32[72,4096]{1,0:T(8,128)} collective-permute-done((f32[72,4096]{1,0:T(8,128)}, f32[72,4096]{1,0:T(8,128)}, u32[]{:S(2)}, u32[]{:S(2)}) %collective-permute-start.12) | collective-permute-done | bytes 1179680 | tf_op jit(solution)/shard_map/ppermute | solution.py:128
  223.0 4.1 collective-permute-done.6
  228.5 2.3 collective-permute-start.22
  230.8 35.3 %shard_map.38.acc_ref = f32[2048,4096]{1,0:T(8,128)} custom-call(bf16[2048,864]{1,0:T(8,128)(2,1)S(1)} %copy-done.1, bf16[864,4096]{1,0:T(8,128)(2,1)} %pad_maximum_fusion.3.b_ref, f32[2048,4096]{1,0:T(8,128)} %shard_map.37.acc_ref), custom_call_target="tpu_custom_call", output_to_operand_aliasing={{}: (2, {})} | custom-call | flops 14495514624 | bytes 77725696 | tf_op jit(solution)/shard_map/pallas_call | solution.py:39
  268.2 2.4 constant_dynamic-update-slice_fusion.5
  270.6 2.4 constant_dynamic-update-slice_fusion.4
  272.9 3.2 fusion.13
  276.2 3.4 pad_maximum_fusion.2.b_ref
  281.0 10.5 %collective-permute-done.13 = f32[72,4096]{1,0:T(8,128)} collective-permute-done((f32[72,4096]{1,0:T(8,128)}, f32[72,4096]{1,0:T(8,128)}, u32[]{:S(2)}, u32[]{:S(2)}) %collective-permute-start.13) | collective-permute-done | bytes 1179680 | tf_op jit(solution)/shard_map/ppermute | solution.py:128
  291.6 1.4 collective-permute-done.7
  293.0 2.3 fusion.26
  295.3 2.4 collective-permute-start.14
  297.8 2.5 constant_dynamic-update-slice_fusion.3
  300.3 2.0 collective-permute-start.17
  302.4 2.4 constant_dynamic-update-slice_fusion.2
  305.9 4.1 copy.16.a_ref
  310.7 1.4 broadcast_select_fusion.9
  313.5 10.2 %collective-permute-done.16 = f32[72,4096]{1,0:T(8,128)} collective-permute-done((f32[72,4096]{1,0:T(8,128)}, f32[72,4096]{1,0:T(8,128)}, u32[]{:S(2)}, u32[]{:S(2)}) %collective-permute-start.16) | collective-permute-done | bytes 1179680 | tf_op jit(solution)/shard_map/ppermute | solution.py:127
  323.7 4.1 collective-permute-done.17
  329.2 1.6 collective-permute-start.18
  330.8 2.4 constant_dynamic-update-slice_fusion.1
  333.1 2.4 constant_dynamic-update-slice_fusion
  335.5 35.3 %shard_map.39.acc_ref = f32[2048,4096]{1,0:T(8,128)} custom-call(bf16[2048,864]{1,0:T(8,128)(2,1)S(1)} %copy-done, bf16[864,4096]{1,0:T(8,128)(2,1)} %pad_maximum_fusion.2.b_ref, f32[2048,4096]{1,0:T(8,128)} %shard_map.38.acc_ref), custom_call_target="tpu_custom_call", output_to_operand_aliasing={{}: (2, {})} | custom-call | flops 14495514624 | bytes 77725696 | tf_op jit(solution)/shard_map/pallas_call | solution.py:39
  372.3 3.2 fusion.12
  375.6 3.4 pad_maximum_fusion.1.b_ref
  380.2 4.1 copy.17.a_ref
  384.3 2.0 copy-done.2
  386.3 35.3 %shard_map.40 = f32[2048,4096]{1,0:T(8,128)} custom-call(bf16[2048,864]{1,0:T(8,128)(2,1)S(1)} %copy-done.2, bf16[864,4096]{1,0:T(8,128)(2,1)} %pad_maximum_fusion.1.b_ref, f32[2048,4096]{1,0:T(8,128)} %shard_map.39.acc_ref), custom_call_target="tpu_custom_call", output_to_operand_aliasing={{}: (2, {})} | custom-call | flops 14495514624 | bytes 77725696 | tf_op jit(solution)/shard_map/pallas_call | solution.py:39
  (84 shorter events, 28.9 us)
Async XLA Ops:
  7.3 6.1 %copy-start.5 = (s32[256]{0:T(256)}, s32[256]{0:T(256)S(1)}, u32[]{:S(2)}) copy-start(s32[256]{0:T(256)S(1)} %select_reduce_fusion) | copy-start | bytes 3076
  8.7 4.7 %copy-start.7 = (f32[256]{0:T(256)}, f32[256]{0:T(256)S(1)}, u32[]{:S(2)}) copy-start(f32[256]{0:T(256)S(1)} %multiply_sqrt_fusion) | copy-start | bytes 3076
  15.0 9.1 %copy-start.9 = (s32[256]{0:T(256)S(1)}, s32[256]{0:T(256)}, u32[]{:S(2)}) copy-start(s32[256]{0:T(256)} %param.7) | copy-start | bytes 3076
  15.0 39.2 %collective-permute-start.2 = (f32[72,4096]{1,0:T(8,128)}, f32[72,4096]{1,0:T(8,128)S(1)}, u32[]{:S(2)}, u32[]{:S(2)}) collective-permute-start(f32[72,4096]{1,0:T(8,128)} %get-tuple-element.173), channel_id=1, source_target_pairs={{0,8},{8,16},{16,24},{24,28},{28,20},{20,12},{12,4},{4,0},{1,9},{9... | collective-permute-start | bytes 3538952 | tf_op jit(solution)/shard_map/ppermute | solution.py:127
  18.1 36.1 %collective-permute-start.8 = (f32[72,4096]{1,0:T(8,128)}, f32[72,4096]{1,0:T(8,128)}, u32[]{:S(2)}, u32[]{:S(2)}) collective-permute-start(f32[72,4096]{1,0:T(8,128)} %get-tuple-element.172), channel_id=1, source_target_pairs={{8,0},{16,8},{24,16},{28,24},{20,28},{12,20},{4,12},{0,4},{9,1},{1... | collective-permute-start | bytes 3538952 | tf_op jit(solution)/shard_map/ppermute | solution.py:128
  19.2 39.7 %collective-permute-start.28 = (f32[144,2048]{1,0:T(8,128)}, f32[144,2048]{1,0:T(8,128)}, u32[]{:S(2)}, u32[]{:S(2)}) collective-permute-start(f32[144,2048]{1,0:T(8,128)} %constant_dynamic-slice_fusion.1), channel_id=1, source_target_pairs={{0,2},{4,6},{9,11},{13,15},{18,16},{22,20},{27,25},{31,29}} | collective-permute-start | bytes 3538952 | tf_op jit(solution)/shard_map/ppermute | solution.py:96
  55.4 17.1 %collective-permute-start.30 = (f32[144,2048]{1,0:T(8,128)S(1)}, f32[144,2048]{1,0:T(8,128)S(1)}, u32[]{:S(2)}, u32[]{:S(2)}) collective-permute-start(f32[144,2048]{1,0:T(8,128)S(1)} %fusion.20), channel_id=1, source_target_pairs={{0,2},{4,6},{9,11},{13,15},{18,16},{22,20},{27,25},{31,29}} | collective-permute-start | bytes 3538952 | tf_op jit(solution)/shard_map/ppermute | solution.py:96
  59.0 37.3 %collective-permute-start.29 = (f32[144,2048]{1,0:T(8,128)S(1)}, f32[144,2048]{1,0:T(8,128)S(1)}, u32[]{:S(2)}, u32[]{:S(2)}) collective-permute-start(f32[144,2048]{1,0:T(8,128)S(1)} %broadcast_select_fusion.3), channel_id=1, source_target_pairs={{0,1},{2,3},{4,5},{6,7},{9,8},{11,10},{13,12},{15,14},{16,17},{18,... | collective-permute-start | bytes 3538952 | tf_op jit(solution)/shard_map/ppermute | solution.py:96
  60.4 24.6 %collective-permute-start.9 = (f32[72,4096]{1,0:T(8,128)}, f32[72,4096]{1,0:T(8,128)}, u32[]{:S(2)}, u32[]{:S(2)}) collective-permute-start(f32[72,4096]{1,0:T(8,128)} %collective-permute-done.8), channel_id=1, source_target_pairs={{8,0},{16,8},{24,16},{28,24},{20,28},{12,20},{4,12},{0,4},{9,1},{1... | collective-permute-start | bytes 3538952 | tf_op jit(solution)/shard_map/ppermute | solution.py:128
  60.7 24.3 %collective-permute-start.3 = (f32[72,4096]{1,0:T(8,128)S(1)}, f32[72,4096]{1,0:T(8,128)}, u32[]{:S(2)}, u32[]{:S(2)}) collective-permute-start(f32[72,4096]{1,0:T(8,128)S(1)} %collective-permute-done.2), channel_id=1, source_target_pairs={{0,8},{8,16},{16,24},{24,28},{28,20},{20,12},{12,4},{4,0},{1,9},{9... | collective-permute-start | bytes 3538952 | tf_op jit(solution)/shard_map/ppermute | solution.py:127
  72.6 26.2 %collective-permute-start.31 = (f32[144,2048]{1,0:T(8,128)S(1)}, f32[144,2048]{1,0:T(8,128)S(1)}, u32[]{:S(2)}, u32[]{:S(2)}) collective-permute-start(f32[144,2048]{1,0:T(8,128)S(1)} %broadcast_select_fusion.2), channel_id=1, source_target_pairs={{0,1},{2,3},{4,5},{6,7},{9,8},{11,10},{13,12},{15,14},{16,17},{18,... | collective-permute-start | bytes 3538952 | tf_op jit(solution)/shard_map/ppermute | solution.py:96
  87.4 37.7 %collective-permute-start.24 = (f32[144,2048]{1,0:T(8,128)}, f32[144,2048]{1,0:T(8,128)}, u32[]{:S(2)}, u32[]{:S(2)}) collective-permute-start(f32[144,2048]{1,0:T(8,128)} %fusion.22), channel_id=1, source_target_pairs={{0,2},{4,6},{9,11},{13,15},{18,16},{22,20},{27,25},{31,29}} | collective-permute-start | bytes 3538952 | tf_op jit(solution)/shard_map/ppermute | solution.py:96
  91.8 27.8 %collective-permute-start.10 = (f32[72,4096]{1,0:T(8,128)}, f32[72,4096]{1,0:T(8,128)}, u32[]{:S(2)}, u32[]{:S(2)}) collective-permute-start(f32[72,4096]{1,0:T(8,128)} %collective-permute-done.9), channel_id=1, source_target_pairs={{8,0},{16,8},{24,16},{28,24},{20,28},{12,20},{4,12},{0,4},{9,1},{1... | collective-permute-start | bytes 3538952 | tf_op jit(solution)/shard_map/ppermute | solution.py:128
  95.9 26.3 %collective-permute-start.4 = (f32[72,4096]{1,0:T(8,128)}, f32[72,4096]{1,0:T(8,128)}, u32[]{:S(2)}, u32[]{:S(2)}) collective-permute-start(f32[72,4096]{1,0:T(8,128)} %collective-permute-done.3), channel_id=1, source_target_pairs={{0,8},{8,16},{16,24},{24,28},{28,20},{20,12},{12,4},{4,0},{1,9},{9... | collective-permute-start | bytes 3538952 | tf_op jit(solution)/shard_map/ppermute | solution.py:127
  122.2 5.7 %copy-start.3 = (bf16[2048,864]{1,0:T(8,128)(2,1)S(1)}, bf16[2048,864]{1,0:T(8,128)(2,1)}, u32[]{:S(2)}) copy-start(bf16[2048,864]{1,0:T(8,128)(2,1)} %copy.14.a_ref) | copy-start | bytes 10616836
  123.7 51.4 %collective-permute-start.26 = (f32[144,2048]{1,0:T(8,128)S(1)}, f32[144,2048]{1,0:T(8,128)S(1)}, u32[]{:S(2)}, u32[]{:S(2)}) collective-permute-start(f32[144,2048]{1,0:T(8,128)S(1)} %fusion.21), channel_id=1, source_target_pairs={{0,2},{4,6},{9,11},{13,15},{18,16},{22,20},{27,25},{31,29}} | collective-permute-start | bytes 3538952 | tf_op jit(solution)/shard_map/ppermute | solution.py:96
  126.5 74.8 %collective-permute-start.25 = (f32[144,2048]{1,0:T(8,128)S(1)}, f32[144,2048]{1,0:T(8,128)S(1)}, u32[]{:S(2)}, u32[]{:S(2)}) collective-permute-start(f32[144,2048]{1,0:T(8,128)S(1)} %broadcast_select_fusion.5), channel_id=1, source_target_pairs={{0,1},{2,3},{4,5},{6,7},{9,8},{11,10},{13,12},{15,14},{16,17},{18,... | collective-permute-start | bytes 3538952 | tf_op jit(solution)/shard_map/ppermute | solution.py:96
  161.4 28.6 %collective-permute-start.11 = (f32[72,4096]{1,0:T(8,128)}, f32[72,4096]{1,0:T(8,128)}, u32[]{:S(2)}, u32[]{:S(2)}) collective-permute-start(f32[72,4096]{1,0:T(8,128)} %collective-permute-done.10), channel_id=1, source_target_pairs={{8,0},{16,8},{24,16},{28,24},{20,28},{12,20},{4,12},{0,4},{9,1},{1... | collective-permute-start | bytes 3538952 | tf_op jit(solution)/shard_map/ppermute | solution.py:128
  163.7 26.4 %collective-permute-start.5 = (f32[72,4096]{1,0:T(8,128)}, f32[72,4096]{1,0:T(8,128)}, u32[]{:S(2)}, u32[]{:S(2)}) collective-permute-start(f32[72,4096]{1,0:T(8,128)} %collective-permute-done.4), channel_id=1, source_target_pairs={{0,8},{8,16},{16,24},{24,28},{28,20},{20,12},{12,4},{4,0},{1,9},{9... | collective-permute-start | bytes 3538952 | tf_op jit(solution)/shard_map/ppermute | solution.py:127
  175.2 28.6 %collective-permute-start.27 = (f32[144,2048]{1,0:T(8,128)S(1)}, f32[144,2048]{1,0:T(8,128)S(1)}, u32[]{:S(2)}, u32[]{:S(2)}) collective-permute-start(f32[144,2048]{1,0:T(8,128)S(1)} %broadcast_select_fusion.4), channel_id=1, source_target_pairs={{0,1},{2,3},{4,5},{6,7},{9,8},{11,10},{13,12},{15,14},{16,17},{18,... | collective-permute-start | bytes 3538952 | tf_op jit(solution)/shard_map/ppermute | solution.py:96
  192.4 17.4 %collective-permute-start.20 = (f32[144,2048]{1,0:T(8,128)}, f32[144,2048]{1,0:T(8,128)}, u32[]{:S(2)}, u32[]{:S(2)}) collective-permute-start(f32[144,2048]{1,0:T(8,128)} %fusion.24), channel_id=1, source_target_pairs={{0,2},{4,6},{9,11},{13,15},{18,16},{22,20},{27,25},{31,29}} | collective-permute-start | bytes 3538952 | tf_op jit(solution)/shard_map/ppermute | solution.py:96
  196.8 26.2 %collective-permute-start.12 = (f32[72,4096]{1,0:T(8,128)}, f32[72,4096]{1,0:T(8,128)}, u32[]{:S(2)}, u32[]{:S(2)}) collective-permute-start(f32[72,4096]{1,0:T(8,128)} %collective-permute-done.11), channel_id=1, source_target_pairs={{8,0},{16,8},{24,16},{28,24},{20,28},{12,20},{4,12},{0,4},{9,1},{1... | collective-permute-start | bytes 3538952 | tf_op jit(solution)/shard_map/ppermute | solution.py:128
  201.1 26.1 %collective-permute-start.6 = (f32[72,4096]{1,0:T(8,128)}, f32[72,4096]{1,0:T(8,128)}, u32[]{:S(2)}, u32[]{:S(2)}) collective-permute-start(f32[72,4096]{1,0:T(8,128)} %collective-permute-done.5), channel_id=1, source_target_pairs={{0,8},{8,16},{16,24},{24,28},{28,20},{20,12},{12,4},{4,0},{1,9},{9... | collective-permute-start | bytes 3538952 | tf_op jit(solution)/shard_map/ppermute | solution.py:127
  209.8 21.0 %copy-start.1 = (bf16[2048,864]{1,0:T(8,128)(2,1)S(1)}, bf16[2048,864]{1,0:T(8,128)(2,1)}, u32[]{:S(2)}) copy-start(bf16[2048,864]{1,0:T(8,128)(2,1)} %copy.15.a_ref) | copy-start | bytes 10616836
  211.4 90.9 %collective-permute-start.21 = (f32[144,2048]{1,0:T(8,128)S(1)}, f32[144,2048]{1,0:T(8,128)S(1)}, u32[]{:S(2)}, u32[]{:S(2)}) collective-permute-start(f32[144,2048]{1,0:T(8,128)S(1)} %broadcast_select_fusion.7), channel_id=1, source_target_pairs={{0,1},{2,3},{4,5},{6,7},{9,8},{11,10},{13,12},{15,14},{16,17},{18,... | collective-permute-start | bytes 3538952 | tf_op jit(solution)/shard_map/ppermute | solution.py:96
  228.5 51.1 %collective-permute-start.22 = (f32[144,2048]{1,0:T(8,128)S(1)}, f32[144,2048]{1,0:T(8,128)S(1)}, u32[]{:S(2)}, u32[]{:S(2)}) collective-permute-start(f32[144,2048]{1,0:T(8,128)S(1)} %fusion.23), channel_id=1, source_target_pairs={{0,2},{4,6},{9,11},{13,15},{18,16},{22,20},{27,25},{31,29}} | collective-permute-start | bytes 3538952 | tf_op jit(solution)/shard_map/ppermute | solution.py:96
  266.2 25.4 %collective-permute-start.13 = (f32[72,4096]{1,0:T(8,128)}, f32[72,4096]{1,0:T(8,128)}, u32[]{:S(2)}, u32[]{:S(2)}) collective-permute-start(f32[72,4096]{1,0:T(8,128)} %collective-permute-done.12), channel_id=1, source_target_pairs={{8,0},{16,8},{24,16},{28,24},{20,28},{12,20},{4,12},{0,4},{9,1},{1... | collective-permute-start | bytes 3538952 | tf_op jit(solution)/shard_map/ppermute | solution.py:128
  266.9 26.0 %collective-permute-start.7 = (f32[72,4096]{1,0:T(8,128)}, f32[72,4096]{1,0:T(8,128)}, u32[]{:S(2)}, u32[]{:S(2)}) collective-permute-start(f32[72,4096]{1,0:T(8,128)} %collective-permute-done.6), channel_id=1, source_target_pairs={{0,8},{8,16},{16,24},{24,28},{28,20},{20,12},{12,4},{4,0},{1,9},{9... | collective-permute-start | bytes 3538952 | tf_op jit(solution)/shard_map/ppermute | solution.py:127
  279.7 25.1 %collective-permute-start.23 = (f32[144,2048]{1,0:T(8,128)S(1)}, f32[144,2048]{1,0:T(8,128)S(1)}, u32[]{:S(2)}, u32[]{:S(2)}) collective-permute-start(f32[144,2048]{1,0:T(8,128)S(1)} %broadcast_select_fusion.6), channel_id=1, source_target_pairs={{0,1},{2,3},{4,5},{6,7},{9,8},{11,10},{13,12},{15,14},{16,17},{18,... | collective-permute-start | bytes 3538952 | tf_op jit(solution)/shard_map/ppermute | solution.py:96
  295.3 15.4 %collective-permute-start.14 = (f32[144,2048]{1,0:T(8,128)}, f32[144,2048]{1,0:T(8,128)}, u32[]{:S(2)}, u32[]{:S(2)}) collective-permute-start(f32[144,2048]{1,0:T(8,128)} %fusion.26), channel_id=1, source_target_pairs={{0,2},{4,6},{9,11},{13,15},{18,16},{22,20},{27,25},{31,29}} | collective-permute-start | bytes 3538952 | tf_op jit(solution)/shard_map/ppermute | solution.py:96
  297.8 26.0 %collective-permute-start.16 = (f32[72,4096]{1,0:T(8,128)}, f32[72,4096]{1,0:T(8,128)}, u32[]{:S(2)}, u32[]{:S(2)}) collective-permute-start(f32[72,4096]{1,0:T(8,128)} %collective-permute-done.7), channel_id=1, source_target_pairs={{0,8},{8,16},{16,24},{24,28},{28,20},{20,12},{12,4},{4,0},{1,9},{9... | collective-permute-start | bytes 3538952 | tf_op jit(solution)/shard_map/ppermute | solution.py:127
  300.3 27.5 %collective-permute-start.17 = (f32[72,4096]{1,0:T(8,128)}, f32[72,4096]{1,0:T(8,128)}, u32[]{:S(2)}, u32[]{:S(2)}) collective-permute-start(f32[72,4096]{1,0:T(8,128)} %collective-permute-done.13), channel_id=1, source_target_pairs={{8,0},{16,8},{24,16},{28,24},{20,28},{12,20},{4,12},{0,4},{9,1},{1... | collective-permute-start | bytes 3538952 | tf_op jit(solution)/shard_map/ppermute | solution.py:128
  312.1 66.8 %collective-permute-start.15 = (f32[144,2048]{1,0:T(8,128)S(1)}, f32[144,2048]{1,0:T(8,128)S(1)}, u32[]{:S(2)}, u32[]{:S(2)}) collective-permute-start(f32[144,2048]{1,0:T(8,128)S(1)} %broadcast_select_fusion.9), channel_id=1, source_target_pairs={{0,1},{2,3},{4,5},{6,7},{9,8},{11,10},{13,12},{15,14},{16,17},{18,... | collective-permute-start | bytes 3538952 | tf_op jit(solution)/shard_map/ppermute | solution.py:96
  329.1 6.4 %copy-start = (bf16[2048,864]{1,0:T(8,128)(2,1)S(1)}, bf16[2048,864]{1,0:T(8,128)(2,1)}, u32[]{:S(2)}) copy-start(bf16[2048,864]{1,0:T(8,128)(2,1)} %copy.16.a_ref) | copy-start | bytes 10616836
  329.2 41.7 %collective-permute-start.18 = (f32[144,2048]{1,0:T(8,128)S(1)}, f32[144,2048]{1,0:T(8,128)S(1)}, u32[]{:S(2)}, u32[]{:S(2)}) collective-permute-start(f32[144,2048]{1,0:T(8,128)S(1)} %fusion.25), channel_id=1, source_target_pairs={{0,2},{4,6},{9,11},{13,15},{18,16},{22,20},{27,25},{31,29}} | collective-permute-start | bytes 3538952 | tf_op jit(solution)/shard_map/ppermute | solution.py:96
  371.0 8.1 %collective-permute-start.19 = (f32[144,2048]{1,0:T(8,128)S(1)}, f32[144,2048]{1,0:T(8,128)S(1)}, u32[]{:S(2)}, u32[]{:S(2)}) collective-permute-start(f32[144,2048]{1,0:T(8,128)S(1)} %broadcast_select_fusion.8), channel_id=1, source_target_pairs={{0,1},{2,3},{4,5},{6,7},{9,8},{11,10},{13,12},{15,14},{16,17},{18,... | collective-permute-start | bytes 3538952 | tf_op jit(solution)/shard_map/ppermute | solution.py:96
  384.3 2.0 copy-start.2
  386.3 35.3 %copy-start.6 = (s32[256]{0:T(256)S(1)}, s32[256]{0:T(256)}, u32[]{:S(2)}) copy-start(s32[256]{0:T(256)} %copy-done.5) | copy-start | bytes 3076
  386.3 35.3 %copy-start.8 = (f32[256]{0:T(256)S(1)}, f32[256]{0:T(256)}, u32[]{:S(2)}) copy-start(f32[256]{0:T(256)} %copy-done.7) | copy-start | bytes 3076
  386.3 35.3 %copy-start.10 = (s32[256]{0:T(256)S(1)}, s32[256]{0:T(256)}, u32[]{:S(2)}) copy-start(s32[256]{0:T(256)} %param.7) | copy-start | bytes 3076
